TPU v7x, 32 devices: a whole 2x2x4 slice. The times are simulated.
32 devices in a mesh: blk: 16 (over z, y, core), head: 2 (over x).
Axes of the slice: x: 2, y: 2, z: 4, core: 2. Of those that a mesh axis runs over, the one named last changes fastest.
Arguments:
- queries: bfloat16 [4096, 1024], P('blk', 'head'), may hold values from -216 to 216
- keys: bfloat16 [4096, 1024], P('blk', 'head'), may hold values from -6 to 6
- values: bfloat16 [4096, 1024], P('blk', 'head'), may hold values from -6 to 6
- group_table: int32 [16, 2], P('blk'), may hold values from 0 to 31, as said below
- doc_ids: int32 [4096], replicated, may hold values from 0 to 15, never falling along the last dimension, each value on 1 to 2048 neighbouring positions
Outputs:
- attended: bfloat16 [4096, 1024], P('blk', 'head')
Inputs may be any that keep to these rules, and one draw needn't show every extreme that they name: group_table[d, 1] = 31 - group_table[d, 0]; the first column holds each of 0 to 15 once. `doc_ids`: document numbers never fall along positions; a document holds at most 2048 positions.
All inputs are finite; a program needn't handle non-finite values.
Results may differ from a plain program's by a relative error of at most 0.0049.
Values may be sent and summed in bfloat16 or wider, within the bound.
A program may use at most 192 MiB of HBM per device.

v0:
```python
import math

import jax
import jax.numpy as jnp
from jax import lax
from jax.sharding import PartitionSpec as P

HEAD_DIM = 128


def shards(queries, keys, values, group_table, doc_ids):
    tok_rows = queries.shape[0]
    group_rows = tok_rows // 2
    head_count = queries.shape[1] // HEAD_DIM
    score_scale = 1.0 / math.sqrt(HEAD_DIM)
    whole_table = lax.all_gather(group_table, "blk", axis=0, tiled=True)
    group_docs = doc_ids.reshape(doc_ids.shape[0] // group_rows, group_rows)
    within = jnp.arange(group_rows, dtype=jnp.int32)
    stored_groups = whole_table.reshape(-1)
    all_key_pos = (stored_groups[:, None] * group_rows + within[None, :]).reshape(-1)
    all_key_doc = group_docs[stored_groups].reshape(-1)
    local_groups = group_table.reshape(-1)
    query_pos = (local_groups[:, None] * group_rows + within[None, :]).reshape(-1)
    query_doc = group_docs[local_groups].reshape(-1)
    query_heads = queries.reshape(tok_rows, head_count, HEAD_DIM)

    def attend_shard(running_state, key_piece, value_piece, offset):
        piece_rows = key_piece.shape[0]
        key_pos = lax.dynamic_slice_in_dim(all_key_pos, offset, piece_rows, 0)
        key_doc = lax.dynamic_slice_in_dim(all_key_doc, offset, piece_rows, 0)
        visible = (query_doc[:, None] == key_doc[None, :]) & (
            key_pos[None, :] <= query_pos[:, None]
        )
        summed, running_max, weight_sum = running_state
        key_heads = key_piece.reshape(piece_rows, head_count, HEAD_DIM)
        value_heads = value_piece.reshape(piece_rows, head_count, HEAD_DIM)
        scores = (
            jnp.einsum("qhd,khd->hqk", query_heads, key_heads, preferred_element_type=jnp.float32)
            * score_scale
        )
        scores = jnp.where(visible[None], scores, -1e30)
        new_max = jnp.maximum(running_max, jnp.max(scores, axis=-1))
        weights = jnp.where(visible[None], jnp.exp(scores - new_max[..., None]), 0.0)
        factor = jnp.exp(running_max - new_max)
        weight_sum = weight_sum * factor + jnp.sum(weights, axis=-1)
        summed = summed * jnp.transpose(factor)[..., None] + jnp.einsum(
            "hqk,khd->qhd",
            weights.astype(jnp.bfloat16),
            value_heads,
            preferred_element_type=jnp.float32,
        )
        return (summed, new_max, weight_sum)

    initial = (
        jnp.zeros((tok_rows, head_count, HEAD_DIM), jnp.float32),
        jnp.full((head_count, tok_rows), -1e30, jnp.float32),
        jnp.zeros((head_count, tok_rows), jnp.float32),
    )
    key_piece = lax.all_gather(keys, "blk", axis=0, tiled=True)
    value_piece = lax.all_gather(values, "blk", axis=0, tiled=True)
    shard_count = key_piece.shape[0] // tok_rows
    key_shards = key_piece.reshape(shard_count, tok_rows, key_piece.shape[1])
    value_shards = value_piece.reshape(shard_count, tok_rows, value_piece.shape[1])
    shard_ids = jnp.arange(shard_count, dtype=jnp.int32)

    def step(state_now, item):
        key_one, value_one, shard_index = item
        start = shard_index * tok_rows
        return (attend_shard(state_now, key_one, value_one, start), None)

    final_state, unused = lax.scan(step, initial, (key_shards, value_shards, shard_ids))
    summed, running_max, weight_sum = final_state
    output = summed / jnp.transpose(weight_sum)[..., None]
    return output.reshape(tok_rows, head_count * HEAD_DIM).astype(jnp.bfloat16)


def solution(mesh):
    in_specs = (P("blk", "head"), P("blk", "head"), P("blk", "head"), P("blk", None), P())
    out_specs = P("blk", "head")
    return jax.shard_map(shards, mesh=mesh, in_specs=in_specs, out_specs=out_specs, check_vma=False)
```

profile of v0, /device:TPU:0, one launch (start us, length us, event | category | flops | bytes accessed | tf_op | source)
XLA Modules:
  0.0 186.2 jit_solution(14628548293793121357)
XLA Ops:
  6.5 0.7 all-gather.4.cloned.1.call-update
  7.3 0.7 all-gather.6.cloned.1.call-update
  8.0 23.3 %all-gather = s32[16,1,2]{2,1,0:T(1,128)S(1)} all-gather(s32[1,1,2]{2,1,0:T(1,128)} %bitcast.68), channel_id=1, replica_groups=mesh['blk'=16,'head'=2] {'blk'}, dimensions={0}, use_global_device_ids=true | all-gather | bytes 136 | tf_op jit(solution)/shard_map/all_gather | solution.py:16
  34.6 1.1 copy.23
  36.6 26.1 %all-gather.4.cloned.1.call-done = bf16[4096,512]{1,0:T(8,128)(2,1)} async-done(((bf16[256,512]{1,0:T(8,128)(2,1)}), bf16[4096,512]{1,0:T(8,128)(2,1)}) %all-gather.4.cloned.1.call-update) | async-done | bytes 4194320 | tf_op jit(solution)/shard_map/all_gather | solution.py:59
  62.7 51.1 %all-gather.6.cloned.1.call-done = bf16[4096,512]{1,0:T(8,128)(2,1)} async-done(((bf16[256,512]{1,0:T(8,128)(2,1)}), bf16[4096,512]{1,0:T(8,128)(2,1)}) %all-gather.6.cloned.1.call-update) | async-done | bytes 4194320 | tf_op jit(solution)/shard_map/all_gather | solution.py:60
  113.8 64.7 %while.15 = (s32[]{:T(128)}, f32[256,4,128]{0,2,1:T(8,128)S(1)}, f32[4,256]{1,0:T(4,128)S(1)}, f32[4,256]{1,0:T(4,128)S(1)}, s32[2,128]{1,0:T(2,128)S(1)}, /*ind...) while((s32[]{:T(128)}, f32[256,4,128]{0,2,1:T(8,128)S(1)}, ...), condition=%wide.region_3.4_spmd.clone, body=%wide.region_0.3_spmd.clone.sunk | while | flops 137173248 | bytes 7415023 | solution.py:71
  115.4 1.1 constant_dynamic-slice_fusion.3
  119.4 1.1 constant_dynamic-slice_fusion.3
  123.5 1.1 constant_dynamic-slice_fusion.3
  127.5 1.1 constant_dynamic-slice_fusion.3
  131.5 1.1 constant_dynamic-slice_fusion.3
  135.6 1.1 constant_dynamic-slice_fusion.3
  139.6 1.1 constant_dynamic-slice_fusion.3
  143.7 1.1 constant_dynamic-slice_fusion.3
  147.7 1.1 constant_dynamic-slice_fusion.3
  151.8 1.1 constant_dynamic-slice_fusion.3
  155.8 1.1 constant_dynamic-slice_fusion.3
  159.8 1.1 constant_dynamic-slice_fusion.3
  163.9 1.1 constant_dynamic-slice_fusion.3
  167.9 1.1 constant_dynamic-slice_fusion.3
  172.0 1.1 constant_dynamic-slice_fusion.3
  176.0 1.1 constant_dynamic-slice_fusion.3
  178.5 0.8 copy.30
  (230 shorter events, 40.3 us)
Async XLA Ops:
  6.5 26.2 %copy-start = (s32[4096]{0:T(1024)S(1)}, s32[4096]{0:T(1024)}, u32[]{:S(2)}) copy-start(s32[4096]{0:T(1024)} %param.11) | copy-start | bytes 49156
  6.5 56.1 %all-gather.4.cloned.1.call-start = ((), (), s32[]{:S(2)}) async-start(), calls=%async_computation | async-start | bytes 4456448 | tf_op jit(solution)/shard_map/all_gather | solution.py:59
  7.3 106.5 %all-gather.6.cloned.1.call-start = ((), (), s32[]{:S(2)}) async-start(), calls=%async_computation.1 | async-start | bytes 4456448 | tf_op jit(solution)/shard_map/all_gather | solution.py:60
Sparse Core Ops, SparseCore 0:
  9.5 53.1 all-gather.3
  64.8 48.8 all-gather.5
where the time goes:
time: 187 us; the launch traced here: 186 us
  waiting for transfers between devices  78.6 us (42%)
  local copies, waits for them, and re-layouts  37.4 us (20%)
  blocking collectives  23.3 us (12%)
  between operations  13.5 us (7%)
  matrix products  12.7 us (7%)
  loops' own time  11.4 us (6%)
  other arithmetic  9.23 us (5%)
    all_gather x1, waiting for transfers between devices, shards(): value_piece = lax.all_gather(values, 'blk', axis=0, tiled=True)  51.1 us
    dynamic_slice x64, local copies, waits for them, and re-layouts, shards(): lax.scan(step, initial, (key_shards, value_shards, shard_ids))  31 us
    all_gather x1, waiting for transfers between devices, shards(): key_piece = lax.all_gather(keys, 'blk', axis=0, tiled=True)  26.1 us
    all_gather x1, blocking collectives, shards(): whole_table = lax.all_gather(group_table, 'blk', axis=0, tiled=True)  23.3 us
    another operation x1, loops' own time, shards(): lax.scan(step, initial, (key_shards, value_shards, shard_ids))  11.4 us
    dot_general x16, matrix products, attend_shard(): jnp.einsum('hqk,khd->qhd', weights.astype(jnp.bfloat16), value_heads, pre...  6.68 us
    dot_general x16, matrix products, attend_shard(): jnp.einsum('qhd,khd->hqk', query_heads, key_heads, preferred_element_type...  6.02 us
  transfers between devices with their start and end apart: 2, of which 2 were waited for; matrix products, arithmetic and copies ran while one was open for 3% of the time, Pallas kernels for 0%

commit v1 on v0

v1 whole, which is shorter than its diff:
```python
import functools
import math

import jax
import jax.numpy as jnp
from jax import lax
from jax.experimental import pallas as pl
from jax.experimental.pallas import tpu as pltpu
from jax.sharding import PartitionSpec as P

HEAD_DIM = 128
CORES = 2
LANES = 2


def attend_kernel(
    line, q_ref, k_ref, v_ref, pos_ref, low_ref, high_ref, out_ref,
    kv, posb, top, total, acc, recv, precv, own_send, own_psend, send, psend,
):
    rows, cols = k_ref.shape
    heads = cols // HEAD_DIM
    group = rows // 2
    factor = math.log2(math.e) / math.sqrt(HEAD_DIM)
    me = lax.axis_index("blk")
    core = lax.rem(me, CORES)
    lane = lax.rem(me // CORES, LANES)
    z = me // (CORES * LANES)

    def index(zz, yy, cc):
        return (zz * LANES + yy) * CORES + cc

    across = index(z, 1 - lane, core)
    partner = index(z, lane, 1 - core)
    ahead = index(z + 1, lane, core)
    behind = index(z - 1, lane, core)
    has_ahead = z + 1 < line
    has_behind = z >= 1

    short = rows // 8
    half = (rows - short) // 2
    pieces = ((0, short), (short, half), (short + half, half))

    barrier = pltpu.get_barrier_semaphore()

    def greet(target):
        pl.semaphore_signal(barrier, inc=1, device_id={"blk": target})

    greet(across)
    greet(partner)
    pl.when(has_ahead)(lambda: greet(ahead))
    pl.when(has_behind)(lambda: greet(behind))
    pl.semaphore_wait(barrier, 2 + has_ahead.astype(jnp.int32) + has_behind.astype(jnp.int32))

    def remote(src, dst, ssem, rsem, target):
        return pltpu.make_async_remote_copy(
            src_ref=src, dst_ref=dst, send_sem=ssem, recv_sem=rsem, device_id={"blk": target}
        )

    def own_copies(piece, kind, target):
        start, size = pieces[piece]
        part = pl.ds(start, size)
        found = [
            remote(k_ref.at[part], kv.at[me, part, pl.ds(0, cols)], own_send.at[piece, 0, kind], recv.at[me, piece], target),
            remote(v_ref.at[part], kv.at[me, part, pl.ds(cols, cols)], own_send.at[piece, 1, kind], recv.at[me, piece], target),
        ]
        if piece == 1:
            found.append(remote(pos_ref, posb.at[me], own_psend.at[kind], precv.at[me], target))
        return found

    def relay_copies(source, piece, kind, target):
        start, size = pieces[piece]
        part = pl.ds(start, size)
        found = [remote(kv.at[source, part], kv.at[source, part], send.at[source, piece, kind], recv.at[source, piece], target)]
        if piece == 1:
            found.append(remote(posb.at[source], posb.at[source], psend.at[source, kind], precv.at[source], target))
        return found

    def start_all(copies):
        for one in copies:
            one.start()

    def end_sends(copies):
        for one in copies:
            one.wait_send()

    def arrived(source, piece):
        for one in relay_copies(source, piece, 0, partner):
            one.wait_recv()

    def own_routes(act):
        for piece in (1, 2, 0):
            act(own_copies(piece, 2, across))
            pl.when(has_ahead)(lambda: act(own_copies(piece, 0, ahead)))
            pl.when(has_behind)(lambda: act(own_copies(piece, 1, behind)))
            act(own_copies(piece, 3, partner))

    directions = ((1, has_ahead, ahead), (-1, has_behind, behind))

    def at_distance(step, run):
        for way, onward, target in directions:
            far = z - way * step
            pl.when((far >= 0) & (far < line))(functools.partial(run, far, onward, target))

    def along(step, act, wait):
        def run(far, onward, target):
            source = index(far, lane, core)
            for piece in (1, 2):
                if wait:
                    arrived(source, piece)
                pl.when(onward)(lambda: act(relay_copies(source, piece, 0, target)))
                act(relay_copies(source, piece, 1, across))
                act(relay_copies(source, piece, 2, partner))
        at_distance(step, run)

    def along_short(step, act, wait):
        def run(far, onward, target):
            for yy in (lane, 1 - lane):
                source = index(far, yy, core)
                if wait:
                    arrived(source, 0)
                pl.when(onward)(lambda: act(relay_copies(source, 0, 0, target)))
                act(relay_copies(source, 0, 2, partner))
        at_distance(step, run)

    def crossed(source, act, wait):
        for piece in (1, 2):
            if wait:
                arrived(source, piece)
            act(relay_copies(source, piece, 2, partner))

    def crossed_here(act, wait):
        if wait:
            arrived(across, 0)
        pl.when(has_ahead)(lambda: act(relay_copies(across, 0, 0, ahead)))
        pl.when(has_behind)(lambda: act(relay_copies(across, 0, 1, behind)))
        act(relay_copies(across, 0, 2, partner))
        crossed(across, act, wait)

    def crossed_far(step, act, wait):
        at_distance(step, lambda far, onward, target: crossed(index(far, 1 - lane, core), act, wait))

    def attend(keys_of, values_of, key_pos):
        low = low_ref[...]
        high = high_ref[...]
        bias = []
        for g in range(2):
            here = key_pos(g)
            bias.append(jnp.where((here >= low) & (here <= high), 0.0, -1e30))
        bias = jnp.concatenate(bias, axis=1)
        for h in range(heads):
            column = pl.ds(h * HEAD_DIM, HEAD_DIM)
            scores = lax.dot_general(
                q_ref[:, column], keys_of(h), (((1,), (1,)), ((), ())), preferred_element_type=jnp.float32
            ) + bias
            before = top[h]
            now = jnp.maximum(before, jnp.max(scores, axis=1, keepdims=True))
            weights = jnp.exp2((scores - jnp.concatenate([now] * (rows // HEAD_DIM), axis=1)) * factor)
            fade = jnp.exp2((before - now) * factor)
            top[h] = now
            total[h] = total[h] * fade + jnp.sum(weights, axis=1, keepdims=True)
            acc[:, column] = acc[:, column] * fade + jnp.dot(
                weights.astype(jnp.bfloat16), values_of(h), preferred_element_type=jnp.float32
            )

    def attend_stored(source):
        attend(
            lambda h: kv[source, :, pl.ds(h * HEAD_DIM, HEAD_DIM)],
            lambda h: kv[source, :, pl.ds(cols + h * HEAD_DIM, HEAD_DIM)],
            lambda g: posb[source, pl.ds(g, 1), :],
        )

    def attend_second(source):
        for piece in range(3):
            arrived(source, piece)
        attend_stored(source)

    def attend_far(step):
        def run(far, onward, target):
            def one(j, carry):
                yy = lax.rem(lane + j, 2)
                attend_stored(index(far, yy, core))
                attend_second(index(far, yy, 1 - core))
                return carry
            lax.fori_loop(0, 2, one, 0)
        at_distance(step, run)

    own_routes(start_all)
    top[...] = jnp.full_like(top, -1e30)
    total[...] = jnp.zeros_like(total)
    acc[...] = jnp.zeros_like(acc)
    attend(
        lambda h: k_ref[:, pl.ds(h * HEAD_DIM, HEAD_DIM)],
        lambda h: v_ref[:, pl.ds(h * HEAD_DIM, HEAD_DIM)],
        lambda g: pos_ref[pl.ds(g, 1), :],
    )
    attend_second(partner)

    along(1, start_all, True)
    crossed_here(start_all, True)
    along_short(1, start_all, True)
    attend_stored(across)
    attend_second(index(z, 1 - lane, 1 - core))

    def loop(step, carry):
        along(step, start_all, True)
        along_short(step, start_all, True)
        crossed_far(step - 1, start_all, True)
        attend_far(step - 1)
        return carry

    lax.fori_loop(2, line + 1, loop, 0)

    for h in range(heads):
        column = pl.ds(h * HEAD_DIM, HEAD_DIM)
        out_ref[:, column] = (acc[:, column] / total[h]).astype(out_ref.dtype)

    own_routes(end_sends)
    crossed_here(end_sends, False)

    def drain(step, carry):
        along(step, end_sends, False)
        along_short(step, end_sends, False)
        crossed_far(step, end_sends, False)
        return carry

    lax.fori_loop(1, line, drain, 0)


def solution(mesh):
    members = mesh.shape["blk"]
    line = members // (CORES * LANES)

    def shards(queries, keys, values, group_table, doc_ids):
        rows, cols = queries.shape
        group = rows // 2
        heads = cols // HEAD_DIM
        within = jnp.arange(group, dtype=jnp.int32)
        groups = group_table.reshape(-1)
        positions = groups[:, None] * group + within[None, :]
        query_pos = positions.reshape(-1)
        query_doc = doc_ids.reshape(-1, group)[groups].reshape(-1)
        first = jnp.sum((doc_ids[None, :] < query_doc[:, None]).astype(jnp.int32), axis=1)
        low = jnp.broadcast_to(first[:, None], (rows, 128))
        high = jnp.broadcast_to(query_pos[:, None], (rows, 128))
        tile = jnp.concatenate([positions] * 4, axis=0)
        vmem = pl.BlockSpec(memory_space=pltpu.VMEM)
        return pl.pallas_call(
            functools.partial(attend_kernel, line),
            out_shape=jax.ShapeDtypeStruct((rows, cols), jnp.bfloat16),
            in_specs=[vmem] * 6,
            out_specs=vmem,
            scratch_shapes=[
                pltpu.VMEM((members, rows, 2 * cols), jnp.bfloat16),
                pltpu.VMEM((members, 8, 128), jnp.int32),
                pltpu.VMEM((heads, rows, HEAD_DIM), jnp.float32),
                pltpu.VMEM((heads, rows, HEAD_DIM), jnp.float32),
                pltpu.VMEM((rows, cols), jnp.float32),
                pltpu.SemaphoreType.DMA((members, 3)),
                pltpu.SemaphoreType.DMA((members,)),
                pltpu.SemaphoreType.DMA((3, 2, 4)),
                pltpu.SemaphoreType.DMA((4,)),
                pltpu.SemaphoreType.DMA((members, 3, 3)),
                pltpu.SemaphoreType.DMA((members, 3)),
            ],
            compiler_params=pltpu.CompilerParams(
                collective_id=0, has_side_effects=True, vmem_limit_bytes=60 * 1024 * 1024
            ),
        )(queries, keys, values, tile, low, high)

    in_specs = (P("blk", "head"), P("blk", "head"), P("blk", "head"), P("blk", None), P())
    return jax.shard_map(shards, mesh=mesh, in_specs=in_specs, out_specs=P("blk", "head"), check_vma=False)
```

time: 187 us -> 65.9 us (0.35)
  waiting for transfers between devices: 78.6 us -> 0 us
  Pallas kernels: 0 us -> 57.8 us
  local copies, waits for them, and re-layouts: 37.4 us -> 4.46 us
  blocking collectives: 23.3 us -> 0 us
  between operations: 13.5 us -> 0.01 us
  matrix products: 12.7 us -> 0 us
  loops' own time: 11.4 us -> 0 us
  other arithmetic: 9.23 us -> 3.27 us
    all_gather x2 -> x0, waiting for transfers between devices: 77.2 us -> none  [the longest x1 51.1 us: shards(): value_piece = lax.all_gather(values, 'blk', axis=0, tiled=True)]
    pallas_call x0 -> x1, Pallas kernels: none -> 57.8 us  [shards(): pl.pallas_call(functools.partial(attend_kernel, line), out_shape=jax.Shap...]
    dynamic_slice x96 -> x0, local copies, waits for them, and re-layouts: 33.4 us -> none  [the longest x64 31 us: shards(): lax.scan(step, initial, (key_shards, value_shards, shard_ids))]
    all_gather x1 -> x0, blocking collectives: 23.3 us -> none  [shards(): whole_table = lax.all_gather(group_table, 'blk', axis=0, tiled=True)]
    dot_general x32 -> x0, matrix products: 12.7 us -> none  [the longest x16 6.68 us: attend_shard(): jnp.einsum('hqk,khd->qhd', weights.astype(jnp.bfloat16), value_heads, pre...]
    another operation x1 -> x0, loops' own time: 11.4 us -> none  [shards(): lax.scan(step, initial, (key_shards, value_shards, shard_ids))]
    and x16 -> x0, other arithmetic: 2.19 us -> none  [attend_shard(): (query_doc[:, None] == key_doc[None, :]) & (key_pos[None, :] <= query_pos...]
    reduce_sum x16 -> x1, other arithmetic: 3.33 us -> 1.28 us  [shards(): jnp.sum((doc_ids[None, :] < query_doc[:, None]).astype(jnp.int32), axis=1)]
  transfers between devices with their start and end apart: 2 -> 0, of which waited for: 2 -> 0; matrix products, arithmetic and copies ran while one was open for 3% -> 0% of each run, Pallas kernels for 0% -> 0%
where the time goes in v1:
time: 65.9 us; the launch traced here: 65.6 us
  Pallas kernels  57.8 us (88%)
  local copies, waits for them, and re-layouts  4.46 us (7%)
  other arithmetic  3.27 us (5%)
    pallas_call x1, Pallas kernels, shards(): pl.pallas_call(functools.partial(attend_kernel, line), out_shape=jax.Shap...  57.8 us
    unnamed x1, local copies, waits for them, and re-layouts  1.67 us

profile of v1, /device:TPU:0, one launch (start us, length us, event | category | flops | bytes accessed | tf_op | source)
XLA Modules:
  0.0 65.6 jit_solution(11240537140411149377)
XLA Ops:
  0.0 0.7 %fusion = s32[2]{0:T(128)S(1)} fusion(s32[1,2]{1,0:T(1,128)} %param.8), kind=kLoop, calls=%fused_computation.6 | loop fusion | flops 6 | bytes 16 | tf_op jit(solution)/shard_map/select_n | solution.py:241
  0.7 0.7 %multiply_bitcast_fusion = s32[2]{0:T(128)S(1)} fusion(s32[1,2]{1,0:T(1,128)} %param.8), kind=kLoop, calls=%fused_computation.7 | loop fusion | flops 2 | bytes 16 | tf_op jit(solution)/shard_map/mul | solution.py:239
  1.3 0.1 fusion.1
  1.4 1.3 %gather_fusion = s32[2,128]{1,0:T(2,128)S(1)} fusion(s32[32,128]{1,0:T(8,128)} %bitcast.10, s32[1024]{0:T(1024)S(1)} %pad_clamp_fusion), kind=kCustom, calls=%fused_computation | custom fusion | bytes 2056 | tf_op jit(solution)/shard_map/gather | solution.py:241
  2.7 1.3 %convert_reduce_fusion = s32[256]{0:T(256)S(1)} fusion(s32[4096]{0:T(1024)} %param.9, s32[256]{0:T(256)S(1)} %bitcast.11), kind=kLoop, calls=%fused_computation.1 | loop fusion | flops 3145472 | bytes 18432 | tf_op jit(solution)/shard_map/reduce_sum | solution.py:242
  3.9 0.6 pad_add_fusion.pos_ref
  4.5 0.8 %broadcast_in_dim.4.low_ref = s32[256,128]{1,0:T(8,128)} broadcast(s32[256]{0:T(256)S(1)} %convert_reduce_fusion), dimensions={0} | broadcast | bytes 132096 | tf_op jit(solution)/shard_map/broadcast_in_dim | solution.py:243
  5.3 0.8 %broadcast_in_dim.5.high_ref = s32[256,128]{1,0:T(8,128)} broadcast(s32[256]{0:T(256)S(1)} %get-tuple-element.5), dimensions={0} | broadcast | bytes 132096 | tf_op jit(solution)/shard_map/broadcast_in_dim | solution.py:244
  6.1 57.8 %shard_map.55 = bf16[256,512]{1,0:T(8,128)(2,1)} custom-call(bf16[256,512]{1,0:T(8,128)(2,1)} %q_ref.1, bf16[256,512]{1,0:T(8,128)(2,1)} %k_ref.1, bf16[256,512]{1,0:T(8,128)(2,1)} %v_ref.1, s32[8,128]{1,0:T(8,128)} %pad_add_fusion.pos_ref, s32[256,128]{1,0:T(8,128)} %broadcast_in_dim.4.low_ref, s32[256,128]{1,0:T(8,128)} %broadcast_in_dim.5.high_ref), custom_call_target="tpu_custom_call" | custom-call | tf_op jit(solution)/shard_map/pallas_call | solution.py:247
  63.9 1.7 %copy.7 = bf16[256,512]{1,0:T(8,128)(2,1)} copy(bf16[256,512]{1,0:T(8,128)(2,1)} %shard_map.55) | data formatting | bytes 524288
  (1 shorter events, 0.0 us)

commit v2 on v1

--- a/solution.py
+++ b/solution.py
@@ -14,10 +14,10 @@
 
 
 def attend_kernel(
-    line, q_ref, k_ref, v_ref, pos_ref, low_ref, high_ref, out_ref,
-    kv, posb, top, total, acc, recv, precv, own_send, own_psend, send, psend,
+    line, table_ref, q_hbm, k_hbm, v_hbm, table_hbm, doc_ref, out_ref,
+    kv, posb, q_ref, low_ref, high_ref, top, total, acc, recv, precv, send, psend, load,
 ):
-    rows, cols = k_ref.shape
+    rows, cols = k_hbm.shape
     heads = cols // HEAD_DIM
     group = rows // 2
     factor = math.log2(math.e) / math.sqrt(HEAD_DIM)
@@ -40,6 +40,15 @@
     half = (rows - short) // 2
     pieces = ((0, short), (short, half), (short + half, half))
 
+    loads = (
+        pltpu.make_async_copy(k_hbm, kv.at[me, :, pl.ds(0, cols)], load.at[0]),
+        pltpu.make_async_copy(v_hbm, kv.at[me, :, pl.ds(cols, cols)], load.at[1]),
+        pltpu.make_async_copy(table_hbm, posb.at[me], load.at[2]),
+        pltpu.make_async_copy(q_hbm, q_ref, load.at[3]),
+    )
+    for one in loads:
+        one.start()
+
     barrier = pltpu.get_barrier_semaphore()
 
     def greet(target):
@@ -55,17 +64,6 @@
         return pltpu.make_async_remote_copy(
             src_ref=src, dst_ref=dst, send_sem=ssem, recv_sem=rsem, device_id={"blk": target}
         )
-
-    def own_copies(piece, kind, target):
-        start, size = pieces[piece]
-        part = pl.ds(start, size)
-        found = [
-            remote(k_ref.at[part], kv.at[me, part, pl.ds(0, cols)], own_send.at[piece, 0, kind], recv.at[me, piece], target),
-            remote(v_ref.at[part], kv.at[me, part, pl.ds(cols, cols)], own_send.at[piece, 1, kind], recv.at[me, piece], target),
-        ]
-        if piece == 1:
-            found.append(remote(pos_ref, posb.at[me], own_psend.at[kind], precv.at[me], target))
-        return found
 
     def relay_copies(source, piece, kind, target):
         start, size = pieces[piece]
@@ -89,10 +87,10 @@
 
     def own_routes(act):
         for piece in (1, 2, 0):
-            act(own_copies(piece, 2, across))
-            pl.when(has_ahead)(lambda: act(own_copies(piece, 0, ahead)))
-            pl.when(has_behind)(lambda: act(own_copies(piece, 1, behind)))
-            act(own_copies(piece, 3, partner))
+            act(relay_copies(me, piece, 2, across))
+            pl.when(has_ahead)(lambda: act(relay_copies(me, piece, 0, ahead)))
+            pl.when(has_behind)(lambda: act(relay_copies(me, piece, 1, behind)))
+            act(relay_copies(me, piece, 3, partner))
 
     directions = ((1, has_ahead, ahead), (-1, has_behind, behind))
 
@@ -142,9 +140,10 @@
     def attend(keys_of, values_of, key_pos):
         low = low_ref[...]
         high = high_ref[...]
+        within = lax.broadcasted_iota(jnp.int32, (1, group), 1)
         bias = []
         for g in range(2):
-            here = key_pos(g)
+            here = key_pos(g) * group + within
             bias.append(jnp.where((here >= low) & (here <= high), 0.0, -1e30))
         bias = jnp.concatenate(bias, axis=1)
         for h in range(heads):
@@ -166,7 +165,7 @@
         attend(
             lambda h: kv[source, :, pl.ds(h * HEAD_DIM, HEAD_DIM)],
             lambda h: kv[source, :, pl.ds(cols + h * HEAD_DIM, HEAD_DIM)],
-            lambda g: posb[source, pl.ds(g, 1), :],
+            lambda g: posb[source][:, g:g + 1],
         )
 
     def attend_second(source):
@@ -184,15 +183,27 @@
             lax.fori_loop(0, 2, one, 0)
         at_distance(step, run)
 
+    for one in loads:
+        one.wait()
     own_routes(start_all)
     top[...] = jnp.full_like(top, -1e30)
     total[...] = jnp.zeros_like(total)
     acc[...] = jnp.zeros_like(acc)
-    attend(
-        lambda h: k_ref[:, pl.ds(h * HEAD_DIM, HEAD_DIM)],
-        lambda h: v_ref[:, pl.ds(h * HEAD_DIM, HEAD_DIM)],
-        lambda g: pos_ref[pl.ds(g, 1), :],
-    )
+    down = lax.broadcasted_iota(jnp.int32, (group, group), 0)
+    right = lax.broadcasted_iota(jnp.int32, (group, group), 1)
+    for g in range(2):
+        own_group = table_ref[0, g]
+        own_doc = jnp.broadcast_to(doc_ref[pl.ds(own_group, 1), :], (group, group))
+        own_doc = jnp.sum(jnp.where(down == right, own_doc, 0), axis=1, keepdims=True)
+
+        def count(i, found):
+            return found + (doc_ref[pl.ds(i, 1), :] < own_doc).astype(jnp.int32)
+
+        found = lax.fori_loop(0, doc_ref.shape[0], count, jnp.zeros((group, group), jnp.int32))
+        part = pl.ds(g * group, group)
+        low_ref[part, :] = jnp.broadcast_to(jnp.sum(found, axis=1, keepdims=True), (group, group))
+        high_ref[part, :] = own_group * group + down
+    attend_stored(me)
     attend_second(partner)
 
     along(1, start_all, True)
@@ -234,38 +245,32 @@
         rows, cols = queries.shape
         group = rows // 2
         heads = cols // HEAD_DIM
-        within = jnp.arange(group, dtype=jnp.int32)
-        groups = group_table.reshape(-1)
-        positions = groups[:, None] * group + within[None, :]
-        query_pos = positions.reshape(-1)
-        query_doc = doc_ids.reshape(-1, group)[groups].reshape(-1)
-        first = jnp.sum((doc_ids[None, :] < query_doc[:, None]).astype(jnp.int32), axis=1)
-        low = jnp.broadcast_to(first[:, None], (rows, 128))
-        high = jnp.broadcast_to(query_pos[:, None], (rows, 128))
-        tile = jnp.concatenate([positions] * 4, axis=0)
+        doc_rows = doc_ids.reshape(-1, group)
         vmem = pl.BlockSpec(memory_space=pltpu.VMEM)
         return pl.pallas_call(
             functools.partial(attend_kernel, line),
             out_shape=jax.ShapeDtypeStruct((rows, cols), jnp.bfloat16),
-            in_specs=[vmem] * 6,
+            in_specs=[pl.BlockSpec(memory_space=pltpu.SMEM)] + [pl.BlockSpec(memory_space=pl.ANY)] * 4 + [vmem],
             out_specs=vmem,
             scratch_shapes=[
                 pltpu.VMEM((members, rows, 2 * cols), jnp.bfloat16),
-                pltpu.VMEM((members, 8, 128), jnp.int32),
+                pltpu.VMEM((members, 1, 2), jnp.int32),
+                pltpu.VMEM((rows, cols), jnp.bfloat16),
+                pltpu.VMEM((rows, group), jnp.int32),
+                pltpu.VMEM((rows, group), jnp.int32),
                 pltpu.VMEM((heads, rows, HEAD_DIM), jnp.float32),
                 pltpu.VMEM((heads, rows, HEAD_DIM), jnp.float32),
                 pltpu.VMEM((rows, cols), jnp.float32),
                 pltpu.SemaphoreType.DMA((members, 3)),
                 pltpu.SemaphoreType.DMA((members,)),
-                pltpu.SemaphoreType.DMA((3, 2, 4)),
+                pltpu.SemaphoreType.DMA((members, 3, 4)),
+                pltpu.SemaphoreType.DMA((members, 4)),
                 pltpu.SemaphoreType.DMA((4,)),
-                pltpu.SemaphoreType.DMA((members, 3, 3)),
-                pltpu.SemaphoreType.DMA((members, 3)),
             ],
             compiler_params=pltpu.CompilerParams(
                 collective_id=0, has_side_effects=True, vmem_limit_bytes=60 * 1024 * 1024
             ),
-        )(queries, keys, values, tile, low, high)
+        )(group_table, queries, keys, values, group_table, doc_rows)
 
     in_specs = (P("blk", "head"), P("blk", "head"), P("blk", "head"), P("blk", None), P())
     return jax.shard_map(shards, mesh=mesh, in_specs=in_specs, out_specs=P("blk", "head"), check_vma=False)

time: 65.9 us -> 59.4 us (0.901)
  other arithmetic: 3.27 us -> 0 us
  local copies, waits for them, and re-layouts: 4.46 us -> 1.67 us
    broadcast_in_dim x2 -> x0, local copies, waits for them, and re-layouts: 1.51 us -> none  [the longest x1 0.76 us: shards(): high = jnp.broadcast_to(query_pos[:, None], (rows, 128))]
    reduce_sum x1 -> x0, other arithmetic: 1.28 us -> none  [shards(): jnp.sum((doc_ids[None, :] < query_doc[:, None]).astype(jnp.int32), axis=1)]
    gather x1 -> x0, local copies, waits for them, and re-layouts: 1.27 us -> none  [shards(): query_doc = doc_ids.reshape(-1, group)[groups].reshape(-1)]
where the time goes in v2:
time: 59.4 us; the launch traced here: 59.2 us
  Pallas kernels  57.5 us (97%)
  local copies, waits for them, and re-layouts  1.67 us (3%)
    pallas_call x1, Pallas kernels, shards(): pl.pallas_call(functools.partial(attend_kernel, line), out_shape=jax.Shap...  57.5 us
    unnamed x1, local copies, waits for them, and re-layouts  1.67 us

profile of v2, /device:TPU:0, one launch (start us, length us, event | category | flops | bytes accessed | tf_op | source)
XLA Modules:
  0.0 59.2 jit_solution(11956328726475733712)
XLA Ops:
  0.0 57.5 %shard_map.55 = bf16[256,512]{1,0:T(8,128)(2,1)} custom-call(s32[1,2]{1,0:T(1,128)} %table_hbm.1, bf16[256,512]{1,0:T(8,128)(2,1)} %q_hbm.1, bf16[256,512]{1,0:T(8,128)(2,1)} %k_hbm.1, bf16[256,512]{1,0:T(8,128)(2,1)} %v_hbm.1, s32[1,2]{1,0:T(1,128)} %table_hbm.1, s32[32,128]{1,0:T(8,128)} %bitcast.1), custom_call_target="tpu_custom_call" | custom-call | tf_op jit(solution)/shard_map/pallas_call | solution.py:250
  57.5 1.7 %copy.7 = bf16[256,512]{1,0:T(8,128)(2,1)} copy(bf16[256,512]{1,0:T(8,128)(2,1)} %shard_map.55) | data formatting | bytes 524288

commit v3 on v2

--- a/solution.py
+++ b/solution.py
@@ -86,7 +86,7 @@
             one.wait_recv()
 
     def own_routes(act):
-        for piece in (1, 2, 0):
+        for piece in (0, 1, 2):
             act(relay_copies(me, piece, 2, across))
             pl.when(has_ahead)(lambda: act(relay_copies(me, piece, 0, ahead)))
             pl.when(has_behind)(lambda: act(relay_copies(me, piece, 1, behind)))
@@ -126,13 +126,12 @@
                 arrived(source, piece)
             act(relay_copies(source, piece, 2, partner))
 
-    def crossed_here(act, wait):
+    def crossed_short(act, wait):
         if wait:
             arrived(across, 0)
         pl.when(has_ahead)(lambda: act(relay_copies(across, 0, 0, ahead)))
         pl.when(has_behind)(lambda: act(relay_copies(across, 0, 1, behind)))
         act(relay_copies(across, 0, 2, partner))
-        crossed(across, act, wait)
 
     def crossed_far(step, act, wait):
         at_distance(step, lambda far, onward, target: crossed(index(far, 1 - lane, core), act, wait))
@@ -204,10 +203,11 @@
         low_ref[part, :] = jnp.broadcast_to(jnp.sum(found, axis=1, keepdims=True), (group, group))
         high_ref[part, :] = own_group * group + down
     attend_stored(me)
+    crossed_short(start_all, True)
     attend_second(partner)
 
     along(1, start_all, True)
-    crossed_here(start_all, True)
+    crossed(across, start_all, True)
     along_short(1, start_all, True)
     attend_stored(across)
     attend_second(index(z, 1 - lane, 1 - core))
@@ -226,7 +226,8 @@
         out_ref[:, column] = (acc[:, column] / total[h]).astype(out_ref.dtype)
 
     own_routes(end_sends)
-    crossed_here(end_sends, False)
+    crossed_short(end_sends, False)
+    crossed(across, end_sends, False)
 
     def drain(step, carry):
         along(step, end_sends, False)

time: 59.4 us -> 56.7 us (0.955)
  Pallas kernels: 57.5 us -> 54.8 us
    pallas_call x1, Pallas kernels: 57.5 us -> 54.8 us  [shards(): pl.pallas_call(functools.partial(attend_kernel, line), out_shape=jax.Shap...]
where the time goes in v3:
time: 56.7 us; the launch traced here: 56.4 us
  Pallas kernels  54.8 us (97%)
  local copies, waits for them, and re-layouts  1.67 us (3%)
    pallas_call x1, Pallas kernels, shards(): pl.pallas_call(functools.partial(attend_kernel, line), out_shape=jax.Shap...  54.8 us
    unnamed x1, local copies, waits for them, and re-layouts  1.67 us

profile of v3, /device:TPU:0, one launch (start us, length us, event | category | flops | bytes accessed | tf_op | source)
XLA Modules:
  0.0 56.4 jit_solution(910981080922516753)
XLA Ops:
  0.0 54.8 %shard_map.55 = bf16[256,512]{1,0:T(8,128)(2,1)} custom-call(s32[1,2]{1,0:T(1,128)} %table_hbm.1, bf16[256,512]{1,0:T(8,128)(2,1)} %q_hbm.1, bf16[256,512]{1,0:T(8,128)(2,1)} %k_hbm.1, bf16[256,512]{1,0:T(8,128)(2,1)} %v_hbm.1, s32[1,2]{1,0:T(1,128)} %table_hbm.1, s32[32,128]{1,0:T(8,128)} %bitcast.1), custom_call_target="tpu_custom_call" | custom-call | tf_op jit(solution)/shard_map/pallas_call | solution.py:251
  54.8 1.7 %copy.7 = bf16[256,512]{1,0:T(8,128)(2,1)} copy(bf16[256,512]{1,0:T(8,128)(2,1)} %shard_map.55) | data formatting | bytes 524288
